TPU v7x, 32 devices: a whole 2x2x4 slice. The times are simulated.
32 devices in a mesh: gz: 16 (over z, y, core), ba: 2 (over x).
Axes of the slice: x: 2, y: 2, z: 4, core: 2. Of those that a mesh axis runs over, the one named last changes fastest.
Arguments:
- coeffs: float32 [2, 3, 4, 32, 128, 128], P(None, None, 'ba', 'gz'), may hold values from -6 to 6
- material: int32 [32, 128, 128], P('gz'), may hold values from 0 to 3
- inv_diag: float32 [4, 3], replicated, may hold values from 0.1 to 1
- inv_off: float32 [4, 3], replicated, may hold values from -0.1 to 0.1
Outputs:
- theta: float32 [2, 3, 4, 32, 128, 128], P(None, None, 'ba', 'gz')
- gram: float32 [2, 4, 4], P(None, None, 'ba')
Inputs may be any that keep to these rules, and one draw needn't show every extreme that they name: material indices.
All inputs are finite; a program needn't handle non-finite values.
Results may differ from a plain program's by a relative error of at most 0.00011.
Values sent between devices are 32-bit elements; how exact they have to be, the bound alone decides.
A program may use at most 64 MiB of HBM per device.

v0:
```python
import functools
import math

import jax
import jax.numpy as jnp
import numpy as np
from jax import lax
from jax.experimental import pallas as pl
from jax.experimental.pallas import tpu as pltpu
from jax.sharding import PartitionSpec as P

highest = lax.Precision.HIGHEST
half_turn = 3.141592653589793


def reverse_bits(values, levels):
    flipped = jnp.zeros_like(values)
    for position in range(levels):
        flipped = flipped + (values >> position & 1) * (1 << levels - 1 - position)
    return flipped


def signed_wave(numbers, length):
    shifted = jnp.where(numbers < length // 2, numbers, numbers - length)
    return shifted.astype(jnp.float32) / (length / 2.0)


def phase_tables(first, second, length, sign):
    product = first[:, None] * second[None, :] % length
    angle = 2.0 * half_turn / length * product.astype(jnp.float32)
    factor = 1.0 / math.sqrt(length)
    return (jnp.cos(angle) * factor, sign * jnp.sin(angle) * factor)


def cross_waves(waves, field):
    first, second, third = waves
    return jnp.stack(
        [
            second * field[:, 2] - third * field[:, 1],
            third * field[:, 0] - first * field[:, 2],
            first * field[:, 1] - second * field[:, 0],
        ],
        axis=1,
    )


def along_width(field, cosine, sine):
    breadth = field.shape[-1]
    rows = field.reshape(2, -1, breadth)
    joined = jnp.concatenate([cosine, sine], axis=1)
    real_prod = jnp.dot(rows[0], joined, precision=highest)
    imag_prod = jnp.dot(rows[1], joined, precision=highest)
    real_out = real_prod[:, :breadth] - imag_prod[:, breadth:]
    imag_out = real_prod[:, breadth:] + imag_prod[:, :breadth]
    return jnp.stack([real_out, imag_out]).reshape(field.shape)


def along_height(field, cosine, sine):
    tables = jnp.stack([cosine, sine])
    product = jnp.einsum("pcbzyx,tyk->tpcbzkx", field, tables, precision=highest)
    return jnp.stack([product[0, 0] - product[1, 1], product[1, 0] + product[0, 1]])


def along_depth(field, cosine, sine):
    tables = jnp.stack([cosine, sine])
    product = jnp.einsum("pcbzyx,tzk->tpcbkyx", field, tables, precision=highest)
    return jnp.stack([product[0, 0] - product[1, 1], product[1, 0] + product[0, 1]])


def apply_material(field, material, inv_diag, inv_off):
    materials = inv_diag.shape[0]
    onehot = (material[None] == jnp.arange(materials, dtype=jnp.int32)[:, None, None, None]).astype(
        jnp.float32
    )
    table = jnp.concatenate([inv_diag, inv_off], axis=1)
    tensor = jnp.einsum("mk,mzyx->kzyx", table, onehot, precision=highest)
    first = field[:, 0]
    second = field[:, 1]
    third = field[:, 2]
    return jnp.stack(
        [
            tensor[0] * first + tensor[3] * second + tensor[5] * third,
            tensor[3] * first + tensor[1] * second + tensor[4] * third,
            tensor[5] * first + tensor[4] * second + tensor[2] * third,
        ],
        axis=1,
    )


def on_device(coeffs, material, inv_diag, inv_off):
    groups = lax.axis_size("gz")
    levels = groups.bit_length() - 1
    depth = coeffs.shape[3]
    height = coeffs.shape[4]
    breadth = coeffs.shape[5]
    total_depth = depth * groups
    device = lax.axis_index("gz")
    local_rows = jnp.arange(depth, dtype=jnp.int32)
    waves_here = reverse_bits(device, levels) + groups * local_rows
    across = jnp.arange(breadth, dtype=jnp.int32)
    upward = jnp.arange(height, dtype=jnp.int32)
    waves = (
        signed_wave(across, breadth)[None, None, :],
        signed_wave(upward, height)[None, :, None],
        signed_wave(waves_here, total_depth)[:, None, None],
    )
    curl = cross_waves(waves, coeffs)
    all_rows = jnp.arange(total_depth, dtype=jnp.int32)
    wave_rows = reverse_bits(all_rows // depth, levels) + groups * (all_rows % depth)
    height_cos, height_sin = phase_tables(upward, upward, height, 1.0)
    width_cos, width_sin = phase_tables(across, across, breadth, 1.0)
    planar = along_height(curl, height_cos, height_sin)
    planar = along_width(planar, width_cos, width_sin)
    material_slab = lax.all_to_all(material, "gz", split_axis=1, concat_axis=0, tiled=True)
    inverse_cos, inverse_sin = phase_tables(wave_rows, all_rows, total_depth, 1.0)
    forward_cos, forward_sin = phase_tables(all_rows, wave_rows, total_depth, -1.0)
    spatial_piece = along_depth(
        lax.all_to_all(planar, "gz", split_axis=4, concat_axis=3, tiled=True),
        inverse_cos,
        inverse_sin,
    )
    scaled_piece = apply_material(spatial_piece, material_slab, inv_diag, inv_off)
    returned = along_depth(scaled_piece, forward_cos, forward_sin)
    spectral = lax.all_to_all(returned, "gz", split_axis=3, concat_axis=4, tiled=True)
    spectral = along_width(spectral, width_cos, -width_sin)
    spectral = along_height(spectral, height_cos, -height_sin)
    theta = -cross_waves(waves, spectral)
    factor = 1.0 / (breadth * height * total_depth)
    piece = lax.all_gather(coeffs, "ba", axis=2, tiled=True)
    real_part = jnp.einsum("cbzyx,cezyx->be", piece[0], theta[0], precision=highest) + jnp.einsum(
        "cbzyx,cezyx->be", piece[1], theta[1], precision=highest
    )
    imag_part = jnp.einsum("cbzyx,cezyx->be", piece[0], theta[1], precision=highest) - jnp.einsum(
        "cbzyx,cezyx->be", piece[1], theta[0], precision=highest
    )
    block = jnp.stack([real_part, imag_part]) * factor
    gram = lax.psum(block, "gz")
    return (theta, gram)


MESH = pl.DeviceIdType.MESH
single = jnp.float32
half = jnp.bfloat16


def split_table(length, extra):
    numbers = np.arange(length)
    angle = 2.0 * np.pi / length * (numbers[:, None] * numbers[None, :] % length)
    cosine = np.cos(angle) * extra / math.sqrt(length)
    sine = np.sin(angle) * extra / math.sqrt(length)
    inverse = np.block([[cosine, sine], [-sine, cosine]])
    parts = []
    for table in (inverse, inverse.T):
        high = table.astype(np.float32).astype(half)
        low = (table - high.astype(np.float64)).astype(half)
        parts += [high, low]
    return np.stack(parts)


def halves(values):
    high = values.astype(half)
    return high, (values - high.astype(single)).astype(half)


def product(first, second):
    dot = functools.partial(jnp.dot, preferred_element_type=single)
    return dot(first[0], second[0]) + (dot(first[0], second[1]) + dot(first[1], second[0]))


def twiddled(pair, step, span, sign):
    real, imag = pair
    if step == 0:
        return real, imag
    if 2 * step == span:
        return (-imag, real) if sign > 0 else (imag, -real)
    angle = math.pi * step / span
    cosine, sine = math.cos(angle), sign * math.sin(angle)
    return real * cosine - imag * sine, real * sine + imag * cosine


def to_voxels(points):
    points = list(points)
    span = 1
    while span < len(points):
        for base in range(0, len(points), 2 * span):
            for step in range(span):
                a = points[base + step]
                t = twiddled(points[base + step + span], step, span, 1.0)
                points[base + step] = (a[0] + t[0], a[1] + t[1])
                points[base + step + span] = (a[0] - t[0], a[1] - t[1])
        span *= 2
    return points


def to_waves(points):
    points = list(points)
    span = len(points) // 2
    while span >= 1:
        for base in range(0, len(points), 2 * span):
            for step in range(span):
                a, t = points[base + step], points[base + step + span]
                points[base + step] = (a[0] + t[0], a[1] + t[1])
                points[base + step + span] = twiddled(
                    (a[0] - t[0], a[1] - t[1]), step, span, -1.0
                )
        span //= 2
    return points


def operator_kernel(
    groups,
    coeffs_ref,
    material_ref,
    diag_ref,
    off_ref,
    wide_ref,
    tall_ref,
    theta_ref,
    gram_ref,
    other_ref,
    slab_ref,
    tensor_ref,
    high_ref,
    low_ref,
    back_ref,
    field_ref,
    out1_ref,
    in1_ref,
    out2_ref,
    in2_ref,
    sums_ref,
    slab_send,
    slab_recv,
    send1,
    recv1,
    send2,
    recv2,
    other_sem,
    sums_send,
    sums_recv,
):
    _, comps, bands, depth, height, breadth = coeffs_ref.shape
    total = depth * groups
    columns = height // groups
    levels = groups.bit_length() - 1
    me = lax.axis_index("gz")
    mine = lax.axis_index("ba")
    middle = groups // 2

    def offset_of(i):
        away = (i + 1) // 2
        return middle + away - 2 * away * (i % 2)

    def each_peer(body):
        def step(i, carry):
            k = offset_of(i)
            body(k, (me + k) % groups, (me + groups - k) % groups)
            return carry

        lax.fori_loop(0, groups - 1, step, 0)

    barrier = pltpu.get_barrier_semaphore()
    each_peer(
        lambda k, peer, source: pl.semaphore_signal(
            barrier, inc=1, device_id={"gz": peer}, device_id_type=MESH
        )
    )
    pl.semaphore_signal(barrier, inc=1, device_id={"ba": 1 - mine}, device_id_type=MESH)

    across = lax.broadcasted_iota(jnp.int32, (1, breadth), 1)
    upward = lax.broadcasted_iota(jnp.int32, (height, 1), 0)
    wave_x = jnp.where(across < breadth // 2, across, across - breadth).astype(single) / (
        breadth / 2.0
    )
    wave_y = jnp.where(upward < height // 2, upward, upward - height).astype(single) / (
        height / 2.0
    )
    reversed_me = 0
    for position in range(levels):
        reversed_me = reversed_me + (me // (1 << position)) % 2 * (1 << (levels - 1 - position))
    waves_z = []
    for row in range(depth):
        number = reversed_me + groups * row
        signed = number - total * (number // (total // 2))
        waves_z.append(signed.astype(single) / (total / 2.0))

    def cross(parts, row):
        waves = (wave_x, wave_y, waves_z[row])
        return [
            waves[(c + 1) % 3] * parts[(c + 2) % 3] - waves[(c + 2) % 3] * parts[(c + 1) % 3]
            for c in range(3)
        ]

    wide_inv, wide_fwd = (wide_ref[0], wide_ref[1]), (wide_ref[2], wide_ref[3])
    tall_fwd, tall_inv = (tall_ref[0], tall_ref[1]), (tall_ref[2], tall_ref[3])

    def gather_blocks(values):
        top, bottom = values[:height], values[height:]
        return jnp.concatenate(
            [
                jnp.concatenate(
                    [
                        top[:, z * breadth : (z + 1) * breadth],
                        bottom[:, z * breadth : (z + 1) * breadth],
                    ],
                    axis=1,
                )
                for z in range(depth)
            ],
            axis=0,
        )

    def spread_blocks(values):
        return jnp.concatenate(
            [
                jnp.concatenate(
                    [
                        values[z * height : (z + 1) * height, p * breadth : (p + 1) * breadth]
                        for z in range(depth)
                    ],
                    axis=1,
                )
                for p in range(2)
            ],
            axis=0,
        )

    def make_planes(b):
        for p in range(2):
            for z in range(depth):
                curls = cross([coeffs_ref[p, c, b, z] for c in range(3)], z)
                for c in range(3):
                    high, low = halves(curls[c])
                    rows, lanes = pl.ds(p * height, height), pl.ds(z * breadth, breadth)
                    high_ref[c, rows, lanes] = high
                    low_ref[c, rows, lanes] = low

        def one(c, carry):
            tall = product(tall_inv, (high_ref[c], low_ref[c]))
            wide = product(halves(gather_blocks(tall)), wide_inv)
            for p in range(2):
                for z in range(depth):
                    plane = wide[z * height : (z + 1) * height, p * breadth : (p + 1) * breadth]
                    out1_ref[b, :, c, p, z] = plane.reshape(groups, columns, breadth)
            return carry

        lax.fori_loop(0, 3, one, 0)

    def exchange(out, into, send, recv, b, peer, k):
        return pltpu.make_async_remote_copy(
            src_ref=out.at[b, peer],
            dst_ref=into.at[b, me],
            send_sem=send.at[b, k],
            recv_sem=recv.at[b, k],
            device_id={"gz": peer},
            device_id_type=MESH,
        )

    def arrival(out, into, send, recv, b, source, k):
        return pltpu.make_async_remote_copy(
            src_ref=out.at[b, source],
            dst_ref=into.at[b, source],
            send_sem=send.at[b, k],
            recv_sem=recv.at[b, k],
            device_id={"gz": source},
            device_id_type=MESH,
        )

    def start_all(out, into, send, recv, b):
        each_peer(lambda k, peer, source: exchange(out, into, send, recv, b, peer, k).start())
        into[b, me] = out[b, me]

    def finish_all(out, into, send, recv, b):
        each_peer(
            lambda k, peer, source: arrival(out, into, send, recv, b, source, k).wait_recv()
        )

    def drain_all(out, into, send, recv, b):
        each_peer(lambda k, peer, source: exchange(out, into, send, recv, b, peer, k).wait_send())

    def slab_copy(peer, slot, k):
        return pltpu.make_async_remote_copy(
            src_ref=material_ref.at[:, pl.ds(pl.multiple_of(peer * columns, columns), columns), :],
            dst_ref=slab_ref.at[slot],
            send_sem=slab_send.at[k],
            recv_sem=slab_recv.at[k],
            device_id={"gz": peer},
            device_id_type=MESH,
        )

    other_copy = pltpu.make_async_remote_copy(
        src_ref=coeffs_ref,
        dst_ref=other_ref,
        send_sem=other_sem.at[0],
        recv_sem=other_sem.at[1],
        device_id={"ba": 1 - mine},
        device_id_type=MESH,
    )

    make_planes(0)
    pl.semaphore_wait(barrier, groups)
    start_all(out1_ref, in1_ref, send1, recv1, 0)
    each_peer(lambda k, peer, source: slab_copy(peer, me, k).start())
    slab_ref[me] = material_ref[:, pl.ds(pl.multiple_of(me * columns, columns), columns), :]
    other_copy.start()
    for b in range(1, bands):
        make_planes(b)
        start_all(out1_ref, in1_ref, send1, recv1, b)

    each_peer(lambda k, peer, source: slab_copy(source, source, k).wait_recv())
    kinds = diag_ref.shape[0]
    codes = slab_ref[...].reshape(total, columns, breadth)
    for entry in range(6):
        table = diag_ref if entry < 3 else off_ref
        values = jnp.full(codes.shape, table[0, entry % 3], single)
        for kind in range(1, kinds):
            values = jnp.where(codes == kind, table[kind, entry % 3], values)
        tensor_ref[entry] = values

    for b in range(bands):
        finish_all(out1_ref, in1_ref, send1, recv1, b)

        def inverse(c, carry):
            points = [
                (in1_ref[b, r // depth, c, 0, r % depth], in1_ref[b, r // depth, c, 1, r % depth])
                for r in range(total)
            ]
            for z, (real, imag) in enumerate(to_voxels(points)):
                field_ref[c, 0, z] = real
                field_ref[c, 1, z] = imag
            return carry

        lax.fori_loop(0, 3, inverse, 0)

        def scale(z, carry):
            xx, yy, zz, xy, yz, zx = [tensor_ref[entry, z] for entry in range(6)]
            for p in range(2):
                first, second, third = [field_ref[c, p, z] for c in range(3)]
                field_ref[0, p, z] = xx * first + xy * second + zx * third
                field_ref[1, p, z] = xy * first + yy * second + yz * third
                field_ref[2, p, z] = zx * first + yz * second + zz * third
            return carry

        lax.fori_loop(0, total, scale, 0, unroll=4)

        def forward(c, carry):
            points = [(field_ref[c, 0, z], field_ref[c, 1, z]) for z in range(total)]
            for r, (real, imag) in enumerate(to_waves(points)):
                out2_ref[b, r // depth, c, 0, r % depth] = real
                out2_ref[b, r // depth, c, 1, r % depth] = imag
            return carry

        lax.fori_loop(0, 3, forward, 0)
        start_all(out2_ref, in2_ref, send2, recv2, b)

    other_copy.wait()

    def fold(values):
        return jnp.sum(values.reshape(height // 8, 8, breadth), axis=0)

    rows_of = []
    for b in range(bands):
        finish_all(out2_ref, in2_ref, send2, recv2, b)

        def plane_of(c, carry):
            planes = jnp.concatenate(
                [
                    jnp.concatenate(
                        [in2_ref[b, :, c, p, z].reshape(height, breadth) for p in range(2)], axis=1
                    )
                    for z in range(depth)
                ],
                axis=0,
            )
            wide = product(halves(planes), wide_fwd)
            back_ref[c] = product(tall_fwd, halves(spread_blocks(wide)))
            return carry

        lax.fori_loop(0, 3, plane_of, 0)

        for z in range(depth):
            for p in range(2):
                rows, lanes = pl.ds(p * height, height), pl.ds(z * breadth, breadth)
                crossed = cross([back_ref[c, rows, lanes] for c in range(3)], z)
                for c in range(3):
                    theta_ref[p, c, b, z] = -crossed[c]

        def partial(source, a):
            def one(n, sums):
                c, z = n // depth, n % depth
                real, imag = source[0, c, a, z], source[1, c, a, z]
                t_real, t_imag = theta_ref[0, c, b, z], theta_ref[1, c, b, z]
                return (
                    sums[0] + fold(real * t_real + imag * t_imag),
                    sums[1] + fold(real * t_imag - imag * t_real),
                )

            zero = jnp.zeros((8, breadth), single)
            return lax.fori_loop(0, 3 * depth, one, (zero, zero))

        for source in (coeffs_ref, other_ref):
            for a in range(bands):
                for value in partial(source, a):
                    rows_of.append(jnp.sum(value, axis=0, keepdims=True))

    sums_ref[me] = jnp.concatenate(rows_of, axis=0)

    def sums_copy(slot, peer, k):
        return pltpu.make_async_remote_copy(
            src_ref=sums_ref.at[slot],
            dst_ref=sums_ref.at[slot],
            send_sem=sums_send.at[k],
            recv_sem=sums_recv.at[k],
            device_id={"gz": peer},
            device_id_type=MESH,
        )

    each_peer(lambda k, peer, source: sums_copy(me, peer, k).start())
    each_peer(lambda k, peer, source: slab_copy(peer, me, k).wait_send())
    for b in range(bands):
        drain_all(out1_ref, in1_ref, send1, recv1, b)
        drain_all(out2_ref, in2_ref, send2, recv2, b)
    each_peer(lambda k, peer, source: sums_copy(source, source, k).wait_recv())
    gram_ref[...] = jnp.sum(sums_ref[...], axis=0)
    each_peer(lambda k, peer, source: sums_copy(me, peer, k).wait_send())


def on_device_kernel(coeffs, material, inv_diag, inv_off):
    groups = lax.axis_size("gz")
    _, comps, bands, depth, height, breadth = coeffs.shape
    total = depth * groups
    columns = height // groups
    wide = jnp.asarray(split_table(breadth, 1.0 / math.sqrt(total)))
    tall = jnp.asarray(split_table(height, 1.0))
    grams = bands * 4 * bands
    block = (bands, groups, 3, 2, depth, columns, breadth)
    vmem, smem = pl.BlockSpec(memory_space=pltpu.VMEM), pl.BlockSpec(memory_space=pltpu.SMEM)
    dma = pltpu.SemaphoreType.DMA
    theta, sums = pl.pallas_call(
        functools.partial(operator_kernel, groups),
        out_shape=(
            jax.ShapeDtypeStruct(coeffs.shape, single),
            jax.ShapeDtypeStruct((grams, breadth), single),
        ),
        in_specs=[vmem, vmem, smem, smem, vmem, vmem],
        out_specs=(vmem, vmem),
        scratch_shapes=[
            pltpu.VMEM(coeffs.shape, single),
            pltpu.VMEM((groups, depth, columns, breadth), jnp.int32),
            pltpu.VMEM((6, total, columns, breadth), single),
            pltpu.VMEM((3, 2 * height, depth * breadth), half),
            pltpu.VMEM((3, 2 * height, depth * breadth), half),
            pltpu.VMEM((3, 2 * height, depth * breadth), single),
            pltpu.VMEM((3, 2, total, columns, breadth), single),
            pltpu.VMEM(block, single),
            pltpu.VMEM(block, single),
            pltpu.VMEM(block, single),
            pltpu.VMEM(block, single),
            pltpu.VMEM((groups, grams, breadth), single),
            dma((groups,)),
            dma((groups,)),
            dma((bands, groups)),
            dma((bands, groups)),
            dma((bands, groups)),
            dma((bands, groups)),
            dma((2,)),
            dma((groups,)),
            dma((groups,)),
        ],
        compiler_params=pltpu.CompilerParams(
            collective_id=0, has_side_effects=True, vmem_limit_bytes=48 * 1024 * 1024
        ),
        name="maxwell",
    )(coeffs, material, inv_diag, inv_off, wide, tall)
    values = jnp.sum(sums, axis=1) / (breadth * height * total)
    values = values.reshape(bands, 2, bands, 2).transpose(1, 3, 2, 0)
    own, other = values[0], values[1]
    first = lax.axis_index("ba") == 0
    gram = jnp.concatenate([jnp.where(first, own, other), jnp.where(first, other, own)], axis=1)
    return (theta, gram)


def fits(coeffs):
    groups, depth, height, breadth = (
        lax.axis_size("gz"),
        coeffs.shape[3],
        coeffs.shape[4],
        coeffs.shape[5],
    )
    return (
        lax.axis_size("ba") == 2
        and depth == 2
        and height % (8 * groups) == 0
        and height % 128 == 0
        and breadth % 128 == 0
    )


def on_either(coeffs, material, inv_diag, inv_off):
    chosen = on_device_kernel if fits(coeffs) else on_device
    return chosen(coeffs, material, inv_diag, inv_off)


def solution(mesh):
    in_specs = (P(None, None, "ba", "gz", None, None), P("gz", None, None), P(), P())
    out_specs = (P(None, None, "ba", "gz", None, None), P(None, None, "ba"))
    return jax.shard_map(
        on_either, mesh=mesh, in_specs=in_specs, out_specs=out_specs, check_vma=False
    )
```

profile of v0, /device:TPU:0, one launch (start us, length us, event | category | flops | bytes accessed | tf_op | source)
XLA Modules:
  0.0 96.6 jit_solution(7086352370251789888)
XLA Ops:
  0.6 0.0 copy-start
  0.6 1.4 %copy-done = f32[2,3,2,2,128,128]{5,4,3,2,1,0:T(8,128)S(1)} copy-done((f32[2,3,2,2,128,128]{5,4,3,2,1,0:T(8,128)S(1)}, f32[2,3,2,2,128,128]{5,4,3,2,1,0:T(8,128)}, u32[]{:S(2)}) %copy-start) | copy-done | bytes 1572888
  2.0 0.0 copy-start.1
  2.0 1.0 %copy-done.1 = bf16[4,256,256]{2,1,0:T(8,128)(2,1)S(1)} copy-done((bf16[4,256,256]{2,1,0:T(8,128)(2,1)S(1)}, bf16[4,256,256]{2,1,0:T(8,128)(2,1)}, u32[]{:S(2)}) %copy-start.1) | copy-done | bytes 524312
  3.1 0.0 copy-start.2
  3.1 1.0 %copy-done.2 = bf16[4,256,256]{2,1,0:T(8,128)(2,1)S(1)} copy-done((bf16[4,256,256]{2,1,0:T(8,128)(2,1)S(1)}, bf16[4,256,256]{2,1,0:T(8,128)(2,1)}, u32[]{:S(2)}) %copy-start.2) | copy-done | bytes 524312
  4.1 0.0 copy-start.3
  4.1 0.9 copy-done.3
  5.0 0.0 copy-start.4
  5.0 0.7 copy-done.4
  5.7 0.0 copy-start.5
  5.7 0.7 copy-done.5
  6.4 87.9 %maxwell.1 = (f32[2,3,2,2,128,128]{5,4,3,2,1,0:T(8,128)S(1)}, f32[16,128]{1,0:T(8,128)S(1)}) custom-call(f32[2,3,2,2,128,128]{5,4,3,2,1,0:T(8,128)S(1)} %copy-done, s32[2,128,128]{2,1,0:T(8,128)S(1)} %copy-done.3, f32[4,3]{1,0:T(4,128)S(1)} %copy-done.4, f32[4,3]{1,0:T(4,128)S(1)} %copy-done.5, bf16[4,256,256]{2,1,0:T(8,128)(2,1)S(1)} %copy-done.1, ...), custom_call_target="tpu_custom_call" | custom-call | tf_op jit(solution)/shard_map/maxwell/pallas_call | solution.py:539
  94.3 0.1 reduce_sum.9
  94.5 0.1 div.6
  94.6 0.1 copy.8
  94.7 0.1 copy.9
  94.8 0.7 copy.10
  95.5 1.1 %copy.12 = f32[2,3,2,2,128,128]{5,4,3,2,1,0:T(8,128)} copy(f32[2,3,2,2,128,128]{5,4,3,2,1,0:T(8,128)S(1)} %get-tuple-element.12) | data formatting | bytes 3145728
  (3 shorter events, 0.0 us)
Async XLA Ops:
  0.6 1.4 %copy-start = (f32[2,3,2,2,128,128]{5,4,3,2,1,0:T(8,128)S(1)}, f32[2,3,2,2,128,128]{5,4,3,2,1,0:T(8,128)}, u32[]{:S(2)}) copy-start(f32[2,3,2,2,128,128]{5,4,3,2,1,0:T(8,128)} %coeffs_ref.1) | copy-start | bytes 4718596
  2.0 1.0 %copy-start.1 = (bf16[4,256,256]{2,1,0:T(8,128)(2,1)S(1)}, bf16[4,256,256]{2,1,0:T(8,128)(2,1)}, u32[]{:S(2)}) copy-start(bf16[4,256,256]{2,1,0:T(8,128)(2,1)} %constant.15.clone.wide_ref) | copy-start | bytes 1572868
  3.1 1.0 %copy-start.2 = (bf16[4,256,256]{2,1,0:T(8,128)(2,1)S(1)}, bf16[4,256,256]{2,1,0:T(8,128)(2,1)}, u32[]{:S(2)}) copy-start(bf16[4,256,256]{2,1,0:T(8,128)(2,1)} %constant.16.clone.tall_ref) | copy-start | bytes 1572868
  4.1 0.9 copy-start.3
  5.0 0.7 copy-start.4
  5.7 0.7 copy-start.5
where the time goes:
time: 96.9 us; the launch traced here: 96.6 us
  Pallas kernels  87.9 us (91%)
  local copies, waits for them, and re-layouts  7.86 us (8%)
    pallas_call x1, Pallas kernels, on_device_kernel(): pl.pallas_call(functools.partial(operator_kernel, groups), out_shape=(jax...  87.9 us
    unnamed x14, local copies, waits for them, and re-layouts  7.57 us

commit v1 on v0

--- a/solution.py
+++ b/solution.py
@@ -209,33 +209,41 @@
 
 def operator_kernel(
     groups,
+    coeffs_hbm,
+    material_hbm,
+    diag_hbm,
+    off_hbm,
+    table_hbm,
+    theta_ref,
+    gram_ref,
     coeffs_ref,
     material_ref,
+    table_ref,
     diag_ref,
     off_ref,
-    wide_ref,
-    tall_ref,
-    theta_ref,
-    gram_ref,
-    other_ref,
     slab_ref,
     tensor_ref,
     high_ref,
     low_ref,
     back_ref,
     field_ref,
+    scaled_ref,
+    other_ref,
     out1_ref,
     in1_ref,
     out2_ref,
     in2_ref,
     sums_ref,
+    load_sem,
     slab_send,
     slab_recv,
+    half_sem,
     send1,
     recv1,
     send2,
     recv2,
-    other_sem,
+    other_send,
+    other_recv,
     sums_send,
     sums_recv,
 ):
@@ -267,6 +275,16 @@
     )
     pl.semaphore_signal(barrier, inc=1, device_id={"ba": 1 - mine}, device_id_type=MESH)
 
+    loads = [
+        pltpu.make_async_copy(coeffs_hbm, coeffs_ref, load_sem.at[0]),
+        pltpu.make_async_copy(table_hbm, table_ref, load_sem.at[1]),
+        pltpu.make_async_copy(material_hbm, material_ref, load_sem.at[2]),
+        pltpu.make_async_copy(diag_hbm, diag_ref, load_sem.at[3]),
+        pltpu.make_async_copy(off_hbm, off_ref, load_sem.at[4]),
+    ]
+    for load in loads:
+        load.start()
+
     across = lax.broadcasted_iota(jnp.int32, (1, breadth), 1)
     upward = lax.broadcasted_iota(jnp.int32, (height, 1), 0)
     wave_x = jnp.where(across < breadth // 2, across, across - breadth).astype(single) / (
@@ -291,8 +309,11 @@
             for c in range(3)
         ]
 
-    wide_inv, wide_fwd = (wide_ref[0], wide_ref[1]), (wide_ref[2], wide_ref[3])
-    tall_fwd, tall_inv = (tall_ref[0], tall_ref[1]), (tall_ref[2], tall_ref[3])
+    def plain_table():
+        return table_ref[0], table_ref[1]
+
+    def turned_table():
+        return table_ref[2], table_ref[3]
 
     def gather_blocks(values):
         top, bottom = values[:height], values[height:]
@@ -336,8 +357,8 @@
                     low_ref[c, rows, lanes] = low
 
         def one(c, carry):
-            tall = product(tall_inv, (high_ref[c], low_ref[c]))
-            wide = product(halves(gather_blocks(tall)), wide_inv)
+            tall = product(turned_table(), (high_ref[c], low_ref[c]))
+            wide = product(halves(gather_blocks(tall)), plain_table())
             for p in range(2):
                 for z in range(depth):
                     plane = wide[z * height : (z + 1) * height, p * breadth : (p + 1) * breadth]
@@ -378,44 +399,64 @@
     def drain_all(out, into, send, recv, b):
         each_peer(lambda k, peer, source: exchange(out, into, send, recv, b, peer, k).wait_send())
 
+    def columns_of(peer):
+        return pl.ds(pl.multiple_of(peer * columns, columns), columns)
+
     def slab_copy(peer, slot, k):
         return pltpu.make_async_remote_copy(
-            src_ref=material_ref.at[:, pl.ds(pl.multiple_of(peer * columns, columns), columns), :],
-            dst_ref=slab_ref.at[slot],
+            src_ref=material_ref.at[mine, columns_of(peer), :],
+            dst_ref=slab_ref.at[mine, slot],
             send_sem=slab_send.at[k],
             recv_sem=slab_recv.at[k],
             device_id={"gz": peer},
             device_id_type=MESH,
         )
 
-    other_copy = pltpu.make_async_remote_copy(
-        src_ref=coeffs_ref,
-        dst_ref=other_ref,
-        send_sem=other_sem.at[0],
-        recv_sem=other_sem.at[1],
-        device_id={"ba": 1 - mine},
-        device_id_type=MESH,
-    )
-
+    def half_copy(row):
+        return pltpu.make_async_remote_copy(
+            src_ref=slab_ref.at[row],
+            dst_ref=slab_ref.at[row],
+            send_sem=half_sem.at[0],
+            recv_sem=half_sem.at[1],
+            device_id={"ba": 1 - mine},
+            device_id_type=MESH,
+        )
+
+    def other_copy(b):
+        return pltpu.make_async_remote_copy(
+            src_ref=field_ref.at[b],
+            dst_ref=other_ref.at[b],
+            send_sem=other_send.at[b],
+            recv_sem=other_recv.at[b],
+            device_id={"ba": 1 - mine},
+            device_id_type=MESH,
+        )
+
+    loads[0].wait()
+    loads[1].wait()
     make_planes(0)
+    for load in loads[2:]:
+        load.wait()
     pl.semaphore_wait(barrier, groups)
     start_all(out1_ref, in1_ref, send1, recv1, 0)
     each_peer(lambda k, peer, source: slab_copy(peer, me, k).start())
-    slab_ref[me] = material_ref[:, pl.ds(pl.multiple_of(me * columns, columns), columns), :]
-    other_copy.start()
+    slab_ref[mine, me] = material_ref[mine, columns_of(me), :]
     for b in range(1, bands):
         make_planes(b)
         start_all(out1_ref, in1_ref, send1, recv1, b)
 
     each_peer(lambda k, peer, source: slab_copy(source, source, k).wait_recv())
+    half_copy(mine).start()
+    half_copy(1 - mine).wait_recv()
     kinds = diag_ref.shape[0]
-    codes = slab_ref[...].reshape(total, columns, breadth)
-    for entry in range(6):
-        table = diag_ref if entry < 3 else off_ref
-        values = jnp.full(codes.shape, table[0, entry % 3], single)
-        for kind in range(1, kinds):
-            values = jnp.where(codes == kind, table[kind, entry % 3], values)
-        tensor_ref[entry] = values
+    for row in range(depth):
+        codes = slab_ref[row]
+        for entry in range(6):
+            table = diag_ref if entry < 3 else off_ref
+            values = jnp.full(codes.shape, table[0, entry % 3], single)
+            for kind in range(1, kinds):
+                values = jnp.where(codes == kind, table[kind, entry % 3], values)
+            tensor_ref[entry, :, row] = values
 
     for b in range(bands):
         finish_all(out1_ref, in1_ref, send1, recv1, b)
@@ -426,25 +467,28 @@
                 for r in range(total)
             ]
             for z, (real, imag) in enumerate(to_voxels(points)):
-                field_ref[c, 0, z] = real
-                field_ref[c, 1, z] = imag
+                field_ref[b, c, 0, z] = real
+                field_ref[b, c, 1, z] = imag
             return carry
 
         lax.fori_loop(0, 3, inverse, 0)
+        other_copy(b).start()
 
         def scale(z, carry):
-            xx, yy, zz, xy, yz, zx = [tensor_ref[entry, z] for entry in range(6)]
+            xx, yy, zz, xy, yz, zx = [
+                tensor_ref[entry, z // depth, z % depth] for entry in range(6)
+            ]
             for p in range(2):
-                first, second, third = [field_ref[c, p, z] for c in range(3)]
-                field_ref[0, p, z] = xx * first + xy * second + zx * third
-                field_ref[1, p, z] = xy * first + yy * second + yz * third
-                field_ref[2, p, z] = zx * first + yz * second + zz * third
+                first, second, third = [field_ref[b, c, p, z] for c in range(3)]
+                scaled_ref[b, 0, p, z] = xx * first + xy * second + zx * third
+                scaled_ref[b, 1, p, z] = xy * first + yy * second + yz * third
+                scaled_ref[b, 2, p, z] = zx * first + yz * second + zz * third
             return carry
 
         lax.fori_loop(0, total, scale, 0, unroll=4)
 
         def forward(c, carry):
-            points = [(field_ref[c, 0, z], field_ref[c, 1, z]) for z in range(total)]
+            points = [(scaled_ref[b, c, 0, z], scaled_ref[b, c, 1, z]) for z in range(total)]
             for r, (real, imag) in enumerate(to_waves(points)):
                 out2_ref[b, r // depth, c, 0, r % depth] = real
                 out2_ref[b, r // depth, c, 1, r % depth] = imag
@@ -453,13 +497,52 @@
         lax.fori_loop(0, 3, forward, 0)
         start_all(out2_ref, in2_ref, send2, recv2, b)
 
-    other_copy.wait()
-
-    def fold(values):
-        return jnp.sum(values.reshape(height // 8, 8, breadth), axis=0)
-
-    rows_of = []
+    def sums_copy(slot, peer, k):
+        return pltpu.make_async_remote_copy(
+            src_ref=sums_ref.at[slot],
+            dst_ref=sums_ref.at[slot],
+            send_sem=sums_send.at[k],
+            recv_sem=sums_recv.at[k],
+            device_id={"gz": peer},
+            device_id_type=MESH,
+        )
+
+    def make_sums():
+        def add(z, sums):
+            sums = list(sums)
+            for c in range(3):
+                ours = [(scaled_ref[b, c, 0, z], scaled_ref[b, c, 1, z]) for b in range(bands)]
+                fields = [
+                    (source[a, c, 0, z], source[a, c, 1, z])
+                    for source in (field_ref, other_ref)
+                    for a in range(bands)
+                ]
+                n = 0
+                for t_real, t_imag in ours:
+                    for real, imag in fields:
+                        sums[n] = sums[n] + (real * t_real + imag * t_imag)
+                        sums[n + 1] = sums[n + 1] + (real * t_imag - imag * t_real)
+                        n += 2
+            return tuple(sums)
+
+        zero = jnp.zeros((columns, breadth), single)
+        sums = lax.fori_loop(0, total, add, (zero,) * (4 * bands * bands))
+        sums_ref[me] = jnp.concatenate([jnp.sum(v, axis=0, keepdims=True) for v in sums], axis=0)
+
+    half_copy(mine).wait_send()
+    each_peer(lambda k, peer, source: slab_copy(peer, me, k).wait_send())
     for b in range(bands):
+        drain_all(out1_ref, in1_ref, send1, recv1, b)
+
+    for b in range(bands):
+        if b == bands - 1:
+            for a in range(bands):
+                other_copy(a).wait_send()
+                other_copy(a).wait_recv()
+            make_sums()
+            each_peer(lambda k, peer, source: sums_copy(me, peer, k).start())
+            for a in range(b):
+                drain_all(out2_ref, in2_ref, send2, recv2, a)
         finish_all(out2_ref, in2_ref, send2, recv2, b)
 
         def plane_of(c, carry):
@@ -472,8 +555,8 @@
                 ],
                 axis=0,
             )
-            wide = product(halves(planes), wide_fwd)
-            back_ref[c] = product(tall_fwd, halves(spread_blocks(wide)))
+            wide = product(halves(planes), turned_table())
+            back_ref[c] = product(plain_table(), halves(spread_blocks(wide)))
             return carry
 
         lax.fori_loop(0, 3, plane_of, 0)
@@ -485,41 +568,7 @@
                 for c in range(3):
                     theta_ref[p, c, b, z] = -crossed[c]
 
-        def partial(source, a):
-            def one(n, sums):
-                c, z = n // depth, n % depth
-                real, imag = source[0, c, a, z], source[1, c, a, z]
-                t_real, t_imag = theta_ref[0, c, b, z], theta_ref[1, c, b, z]
-                return (
-                    sums[0] + fold(real * t_real + imag * t_imag),
-                    sums[1] + fold(real * t_imag - imag * t_real),
-                )
-
-            zero = jnp.zeros((8, breadth), single)
-            return lax.fori_loop(0, 3 * depth, one, (zero, zero))
-
-        for source in (coeffs_ref, other_ref):
-            for a in range(bands):
-                for value in partial(source, a):
-                    rows_of.append(jnp.sum(value, axis=0, keepdims=True))
-
-    sums_ref[me] = jnp.concatenate(rows_of, axis=0)
-
-    def sums_copy(slot, peer, k):
-        return pltpu.make_async_remote_copy(
-            src_ref=sums_ref.at[slot],
-            dst_ref=sums_ref.at[slot],
-            send_sem=sums_send.at[k],
-            recv_sem=sums_recv.at[k],
-            device_id={"gz": peer},
-            device_id_type=MESH,
-        )
-
-    each_peer(lambda k, peer, source: sums_copy(me, peer, k).start())
-    each_peer(lambda k, peer, source: slab_copy(peer, me, k).wait_send())
-    for b in range(bands):
-        drain_all(out1_ref, in1_ref, send1, recv1, b)
-        drain_all(out2_ref, in2_ref, send2, recv2, b)
+    drain_all(out2_ref, in2_ref, send2, recv2, bands - 1)
     each_peer(lambda k, peer, source: sums_copy(source, source, k).wait_recv())
     gram_ref[...] = jnp.sum(sums_ref[...], axis=0)
     each_peer(lambda k, peer, source: sums_copy(me, peer, k).wait_send())
@@ -530,11 +579,12 @@
     _, comps, bands, depth, height, breadth = coeffs.shape
     total = depth * groups
     columns = height // groups
-    wide = jnp.asarray(split_table(breadth, 1.0 / math.sqrt(total)))
-    tall = jnp.asarray(split_table(height, 1.0))
+    table = jnp.asarray(split_table(breadth, total**-0.25))
     grams = bands * 4 * bands
+    voxels = (bands, 3, 2, total, columns, breadth)
     block = (bands, groups, 3, 2, depth, columns, breadth)
-    vmem, smem = pl.BlockSpec(memory_space=pltpu.VMEM), pl.BlockSpec(memory_space=pltpu.SMEM)
+    vmem = pl.BlockSpec(memory_space=pltpu.VMEM)
+    hbm = pl.BlockSpec(memory_space=pltpu.HBM)
     dma = pltpu.SemaphoreType.DMA
     theta, sums = pl.pallas_call(
         functools.partial(operator_kernel, groups),
@@ -542,28 +592,37 @@
             jax.ShapeDtypeStruct(coeffs.shape, single),
             jax.ShapeDtypeStruct((grams, breadth), single),
         ),
-        in_specs=[vmem, vmem, smem, smem, vmem, vmem],
+        in_specs=[hbm, hbm, hbm, hbm, hbm],
         out_specs=(vmem, vmem),
         scratch_shapes=[
             pltpu.VMEM(coeffs.shape, single),
-            pltpu.VMEM((groups, depth, columns, breadth), jnp.int32),
-            pltpu.VMEM((6, total, columns, breadth), single),
+            pltpu.VMEM(material.shape, jnp.int32),
+            pltpu.VMEM(table.shape, half),
+            pltpu.SMEM(inv_diag.shape, single),
+            pltpu.SMEM(inv_off.shape, single),
+            pltpu.VMEM((depth, groups, columns, breadth), jnp.int32),
+            pltpu.VMEM((6, groups, depth, columns, breadth), single),
             pltpu.VMEM((3, 2 * height, depth * breadth), half),
             pltpu.VMEM((3, 2 * height, depth * breadth), half),
             pltpu.VMEM((3, 2 * height, depth * breadth), single),
-            pltpu.VMEM((3, 2, total, columns, breadth), single),
+            pltpu.VMEM(voxels, single),
+            pltpu.VMEM(voxels, single),
+            pltpu.VMEM(voxels, single),
             pltpu.VMEM(block, single),
             pltpu.VMEM(block, single),
             pltpu.VMEM(block, single),
             pltpu.VMEM(block, single),
             pltpu.VMEM((groups, grams, breadth), single),
+            dma((5,)),
             dma((groups,)),
             dma((groups,)),
+            dma((2,)),
             dma((bands, groups)),
             dma((bands, groups)),
             dma((bands, groups)),
             dma((bands, groups)),
-            dma((2,)),
+            dma((bands,)),
+            dma((bands,)),
             dma((groups,)),
             dma((groups,)),
         ],
@@ -571,7 +630,7 @@
             collective_id=0, has_side_effects=True, vmem_limit_bytes=48 * 1024 * 1024
         ),
         name="maxwell",
-    )(coeffs, material, inv_diag, inv_off, wide, tall)
+    )(coeffs, material, inv_diag, inv_off, table)
     values = jnp.sum(sums, axis=1) / (breadth * height * total)
     values = values.reshape(bands, 2, bands, 2).transpose(1, 3, 2, 0)
     own, other = values[0], values[1]
@@ -591,7 +650,7 @@
         lax.axis_size("ba") == 2
         and depth == 2
         and height % (8 * groups) == 0
-        and height % 128 == 0
+        and height == breadth
         and breadth % 128 == 0
     )
 

time: 96.9 us -> 89.9 us (0.928)
  Pallas kernels: 87.9 us -> 82 us
  local copies, waits for them, and re-layouts: 7.86 us -> 6.82 us
    pallas_call x1, Pallas kernels: 87.9 us -> 82 us  [on_device_kernel(): pl.pallas_call(functools.partial(operator_kernel, groups), out_shape=(jax...]
    unnamed x14 -> x12, local copies, waits for them, and re-layouts: 7.57 us -> 6.53 us
where the time goes in v1:
time: 89.9 us; the launch traced here: 89.6 us
  Pallas kernels  82 us (91%)
  local copies, waits for them, and re-layouts  6.82 us (8%)
    pallas_call x1, Pallas kernels, on_device_kernel(): pl.pallas_call(functools.partial(operator_kernel, groups), out_shape=(jax...  82 us
    unnamed x12, local copies, waits for them, and re-layouts  6.53 us

profile of v1, /device:TPU:0, one launch (start us, length us, event | category | flops | bytes accessed | tf_op | source)
XLA Modules:
  0.0 89.6 jit_solution(490699706279845306)
XLA Ops:
  0.6 0.0 copy-start
  0.6 1.4 %copy-done = f32[2,3,2,2,128,128]{5,4,3,2,1,0:T(8,128)S(1)} copy-done((f32[2,3,2,2,128,128]{5,4,3,2,1,0:T(8,128)S(1)}, f32[2,3,2,2,128,128]{5,4,3,2,1,0:T(8,128)}, u32[]{:S(2)}) %copy-start) | copy-done | bytes 1572888
  2.0 0.0 copy-start.1
  2.0 1.0 %copy-done.1 = bf16[4,256,256]{2,1,0:T(8,128)(2,1)S(1)} copy-done((bf16[4,256,256]{2,1,0:T(8,128)(2,1)S(1)}, bf16[4,256,256]{2,1,0:T(8,128)(2,1)}, u32[]{:S(2)}) %copy-start.1) | copy-done | bytes 524312
  3.1 0.0 copy-start.2
  3.1 0.9 %copy-done.2 = s32[2,128,128]{2,1,0:T(8,128)S(1)} copy-done((s32[2,128,128]{2,1,0:T(8,128)S(1)}, s32[2,128,128]{2,1,0:T(8,128)}, u32[]{:S(2)}) %copy-start.2) | copy-done | bytes 131096
  4.0 0.0 copy-start.3
  4.0 0.7 copy-done.3
  4.7 0.0 copy-start.4
  4.7 0.7 copy-done.4
  5.4 82.0 %maxwell.1 = (f32[2,3,2,2,128,128]{5,4,3,2,1,0:T(8,128)S(1)}, f32[16,128]{1,0:T(8,128)S(1)}) custom-call(f32[2,3,2,2,128,128]{5,4,3,2,1,0:T(8,128)S(1)} %copy-done, s32[2,128,128]{2,1,0:T(8,128)S(1)} %copy-done.2, f32[4,3]{1,0:T(4,128)S(1)} %copy-done.3, f32[4,3]{1,0:T(4,128)S(1)} %copy-done.4, bf16[4,256,256]{2,1,0:T(8,128)(2,1)S(1)} %copy-done.1), custom_call_target="tpu_custom_call" | custom-call | tf_op jit(solution)/shard_map/maxwell/pallas_call | solution.py:589
  87.4 0.1 reduce_sum.9
  87.5 0.1 div.6
  87.6 0.1 copy.7
  87.7 0.1 copy.8
  87.8 0.7 copy.9
  88.5 1.1 %copy.11 = f32[2,3,2,2,128,128]{5,4,3,2,1,0:T(8,128)} copy(f32[2,3,2,2,128,128]{5,4,3,2,1,0:T(8,128)S(1)} %get-tuple-element.12) | data formatting | bytes 3145728
  (3 shorter events, 0.0 us)
Async XLA Ops:
  0.6 1.4 %copy-start = (f32[2,3,2,2,128,128]{5,4,3,2,1,0:T(8,128)S(1)}, f32[2,3,2,2,128,128]{5,4,3,2,1,0:T(8,128)}, u32[]{:S(2)}) copy-start(f32[2,3,2,2,128,128]{5,4,3,2,1,0:T(8,128)} %coeffs_hbm.1) | copy-start | bytes 4718596
  2.0 1.0 %copy-start.1 = (bf16[4,256,256]{2,1,0:T(8,128)(2,1)S(1)}, bf16[4,256,256]{2,1,0:T(8,128)(2,1)}, u32[]{:S(2)}) copy-start(bf16[4,256,256]{2,1,0:T(8,128)(2,1)} %constant.13.clone.table_hbm) | copy-start | bytes 1572868
  3.1 0.9 %copy-start.2 = (s32[2,128,128]{2,1,0:T(8,128)S(1)}, s32[2,128,128]{2,1,0:T(8,128)}, u32[]{:S(2)}) copy-start(s32[2,128,128]{2,1,0:T(8,128)} %material_hbm.1) | copy-start | bytes 393220
  4.0 0.7 copy-start.3
  4.7 0.7 copy-start.4
